TPU v7x, 32 devices: a whole 2x2x4 slice. The times are simulated.
32 devices in a mesh: rows: 16 (over z, y, x), cols: 2 (over core).
Axes of the slice: x: 2, y: 2, z: 4, core: 2. Of those that a mesh axis runs over, the one named last changes fastest.
Arguments:
- eigvecs: float32 [4096, 2048], P('rows', 'cols'), may hold values from -6 to 6
- reflectors: float32 [32, 4096], P('cols', 'rows'), may hold values from -17 to 17
- starts: int32 [32], replicated, may hold values from 0 to 63
Outputs:
- rotated: float32 [4096, 2048], P('rows', 'cols')
Inputs may be any that keep to these rules, and one draw needn't show every extreme that they name: Sweep j's windows begin at rows starts[j] + k * 64.
All inputs are finite; a program needn't handle non-finite values.
Results may differ from a plain program's by a relative error of at most 0.00011.
Values sent between devices are 32-bit elements; how exact they have to be, the bound alone decides.
A program may use at most 64 MiB of HBM per device.

v0:
```python
import jax
import jax.numpy as jnp
from jax import lax
from jax.sharding import PartitionSpec as P

BAND = 64
SWEEPS = 32


def column_sweep(turned, reflector, offset):
    width = turned.shape[0]
    total_rows = turned.shape[1]
    blocks = total_rows // BAND
    rolled = jnp.roll(turned, -offset, axis=1).reshape(width, blocks, BAND)
    rolled_v = jnp.roll(reflector, -offset).reshape(blocks, BAND)
    squares = jnp.sum(rolled_v * rolled_v, axis=1)
    window = jnp.arange(blocks, dtype=jnp.int32)
    usable = (window + 1) * BAND + offset <= total_rows
    scaled = jnp.where(usable, 2.0 / jnp.where(usable, squares, 1.0), 0.0)
    products = jnp.sum(rolled * rolled_v[None, :, :], axis=2)
    rolled = rolled - (products * scaled[None, :])[:, :, None] * rolled_v[None, :, :]
    return jnp.roll(rolled.reshape(width, total_rows), offset, axis=1)


def per_device(eigvecs, reflectors, starts):
    every_sweep = lax.all_gather(reflectors, "cols", axis=0, tiled=True)
    turned = lax.all_to_all(eigvecs, "rows", split_axis=1, concat_axis=0, tiled=True)
    whole_v = lax.all_gather(every_sweep, "rows", axis=1, tiled=True)
    crossed = turned.T

    def advance(sweep_idx, state):
        return column_sweep(state, whole_v[sweep_idx], starts[sweep_idx])

    crossed = lax.fori_loop(0, SWEEPS, advance, crossed)
    return lax.all_to_all(crossed.T, "rows", split_axis=0, concat_axis=1, tiled=True)


def solution(mesh):
    in_specs = (P("rows", "cols"), P("cols", "rows"), P())
    out_specs = P("rows", "cols")
    return jax.shard_map(
        per_device, mesh=mesh, in_specs=in_specs, out_specs=out_specs, check_vma=False
    )
```

profile of v0, /device:TPU:0, one launch (start us, length us, event | category | flops | bytes accessed | tf_op | source)
XLA Modules:
  0.0 527.9 jit_solution(18121734052208252811)
XLA Ops:
  0.0 2.5 copy.12
  2.5 8.5 %all-to-all-start = ((f32[256,16,64]{0,2,1:T(8,128)}), f32[256,16,64]{0,2,1:T(8,128)S(1)}, u32[]{:S(2)}, u32[]{:S(2)}) async-start(f32[256,16,64]{0,2,1:T(8,128)} %bitcast.2), calls=%async_computation | async-start | bytes 2097152 | tf_op jit(solution)/shard_map/all_to_all | solution.py:27
  12.9 55.0 %all_gather.7 = f32[32,4096]{1,0:T(8,128)} all-gather(f32[32,256]{1,0:T(8,128)S(1)} %all_gather.6), channel_id=1, replica_groups=mesh['rows'=16,'cols'=2] {'rows'}, dimensions={1}, use_global_device_ids=true | all-gather | bytes 557056 | tf_op jit(solution)/shard_map/all_gather | solution.py:28
  68.0 435.8 %while.15 = (s32[]{:T(128)}, f32[64,4096]{1,0:T(8,128)S(1)}, s32[32]{0:T(128)S(1)}, f32[32,4096]{1,0:T(8,128)}, s32[]{:T(128)}, /*index=5*/s32[]{:T(128)}, s32[]{:T(128)}, s32[]{:T(128)}, s32[]{:T(128)}) while((s32[]{:T(128)}, f32[64,4096]{1,0:T(8,128)S(1)}, s32[32]{0:T(128)S(1)}, f32[32,4096]{1,0:T(8,128)}, s32[]{:T(128)}, ...), condition=%wide.region_3.5_spmd, body=%wide.region_0.4_spmd.sunk | while | flops 1847711 | bytes 13845943 | solution.py:34
  72.5 2.0 reshape.75
  86.1 2.0 reshape.75
  99.7 2.0 reshape.75
  113.3 2.0 reshape.75
  126.9 2.0 reshape.75
  140.6 2.0 reshape.75
  154.2 2.0 reshape.75
  167.8 2.0 reshape.75
  181.4 2.0 reshape.75
  195.0 2.0 reshape.75
  208.7 2.0 reshape.75
  222.3 2.0 reshape.75
  235.9 2.0 reshape.75
  249.5 2.0 reshape.75
  263.1 2.0 reshape.75
  276.8 2.0 reshape.75
  290.4 2.0 reshape.75
  304.0 2.0 reshape.75
  317.6 2.0 reshape.75
  331.2 2.0 reshape.75
  344.9 2.0 reshape.75
  358.5 2.0 reshape.75
  372.1 2.0 reshape.75
  385.7 2.0 reshape.75
  399.3 2.0 reshape.75
  453.8 2.0 reshape.75
  494.7 2.0 reshape.75
  503.9 22.7 %all_to_all.38 = f32[16,256,64]{1,2,0:T(8,128)S(1)} all-to-all(f32[16,256,64]{1,2,0:T(8,128)S(1)} %bitcast.23), channel_id=1, replica_groups=mesh['rows'=16,'cols'=2] {'rows'}, dimensions={0} | all-to-all | bytes 2097152 | tf_op jit(solution)/shard_map/all_to_all | solution.py:35
  (430 shorter events, 309.5 us)
Async XLA Ops:
  0.0 11.0 %copy-start = (f32[16,256]{1,0:T(8,128)S(1)}, f32[16,256]{1,0:T(8,128)}, u32[]{:S(2)}) copy-start(f32[16,256]{1,0:T(8,128)} %param.8) | copy-start | bytes 49156
  2.5 65.4 %copy-start.1 = (s32[32]{0:T(128)S(1)}, s32[32]{0:T(128)}, u32[]{:S(2)}) copy-start(s32[32]{0:T(128)} %param.9) | copy-start | bytes 388
  2.5 65.3 %all-to-all-start = ((f32[256,16,64]{0,2,1:T(8,128)}), f32[256,16,64]{0,2,1:T(8,128)S(1)}, u32[]{:S(2)}, u32[]{:S(2)}) async-start(f32[256,16,64]{0,2,1:T(8,128)} %bitcast.2), calls=%async_computation | async-start | bytes 2097152 | tf_op jit(solution)/shard_map/all_to_all | solution.py:27
where the time goes:
time: 532 us; the launch traced here: 528 us
  local copies, waits for them, and re-layouts  190 us (36%)
  other arithmetic  174 us (33%)
  blocking collectives  79.5 us (15%)
  loops' own time  75.8 us (14%)
  starting transfers between devices  8.47 us (2%)
    another operation x1, loops' own time, per_device(): crossed = lax.fori_loop(0, SWEEPS, advance, crossed)  75.8 us
    mul x64, local copies, waits for them, and re-layouts, column_sweep(): (products * scaled[None, :])[:, :, None] * rolled_v[None, :, :]  71.3 us
    reshape x32, local copies, waits for them, and re-layouts, column_sweep(): rolled = jnp.roll(turned, -offset, axis=1).reshape(width, blocks, BAND)  63.9 us
    sub x32, other arithmetic, column_sweep(): rolled - (products * scaled[None, :])[:, :, None] * rolled_v[None, :, :]  58.7 us
    all_gather x1, blocking collectives, per_device(): whole_v = lax.all_gather(every_sweep, 'rows', axis=1, tiled=True)  55 us
    concatenate x32, other arithmetic, column_sweep(): rolled = jnp.roll(turned, -offset, axis=1).reshape(width, blocks, BAND)  50.8 us
    dynamic_slice x64, local copies, waits for them, and re-layouts, advance(): return column_sweep(state, whole_v[sweep_idx], starts[sweep_idx])  48.1 us
    all_to_all x1, blocking collectives, per_device(): lax.all_to_all(crossed.T, 'rows', split_axis=0, concat_axis=1, tiled=True)  22.7 us
  transfers between devices with their start and end apart: 1, of which 0 were waited for; matrix products, arithmetic and copies ran while one was open for 0% of the time, Pallas kernels for 0%

commit v1 on v0

--- a/solution.py
+++ b/solution.py
@@ -25,7 +25,12 @@
 def per_device(eigvecs, reflectors, starts):
     every_sweep = lax.all_gather(reflectors, "cols", axis=0, tiled=True)
     turned = lax.all_to_all(eigvecs, "rows", split_axis=1, concat_axis=0, tiled=True)
-    whole_v = lax.all_gather(every_sweep, "rows", axis=1, tiled=True)
+    ring = [every_sweep]
+    for hop in range(15):
+        ring.append(lax.ppermute(ring[-1], "rows", [(dev, (dev + 1) % 16) for dev in range(16)]))
+    whole_v = jnp.roll(
+        jnp.concatenate(ring[::-1], axis=1), (lax.axis_index("rows") + 1) * ring[0].shape[1], axis=1
+    )
     crossed = turned.T
 
     def advance(sweep_idx, state):

time: 532 us -> 593 us (1.11)
  waiting for transfers between devices: 0.01 us -> 118 us
  blocking collectives: 79.5 us -> 23.8 us
    ppermute x0 -> x15, waiting for transfers between devices: none -> 104 us  [per_device(): lax.ppermute(ring[-1], 'rows', [(dev, (dev + 1) % 16) for dev in range(16)])]
    all_gather x1 -> x0, blocking collectives: 55 us -> none  [per_device(): whole_v = lax.all_gather(every_sweep, 'rows', axis=1, tiled=True)]
    all_to_all x1, waiting for transfers between devices: 0.01 us -> 14.3 us  [per_device(): lax.all_to_all(eigvecs, 'rows', split_axis=1, concat_axis=0, tiled=True)]
  transfers between devices with their start and end apart: 1 -> 16, of which waited for: 0 -> 15; matrix products, arithmetic and copies ran while one was open for 0% -> 1% of each run, Pallas kernels for 0% -> 0%
where the time goes in v1:
time: 593 us; the launch traced here: 589 us
  local copies, waits for them, and re-layouts  190 us (32%)
  other arithmetic  174 us (29%)
  waiting for transfers between devices  118 us (20%)
  loops' own time  73.1 us (12%)
  blocking collectives  23.8 us (4%)
  starting transfers between devices  9.9 us (2%)
    ppermute x15, waiting for transfers between devices, per_device(): lax.ppermute(ring[-1], 'rows', [(dev, (dev + 1) % 16) for dev in range(16)])  104 us
    another operation x1, loops' own time, per_device(): crossed = lax.fori_loop(0, SWEEPS, advance, crossed)  73.1 us
    mul x64, local copies, waits for them, and re-layouts, column_sweep(): (products * scaled[None, :])[:, :, None] * rolled_v[None, :, :]  71.3 us
    reshape x32, local copies, waits for them, and re-layouts, column_sweep(): rolled = jnp.roll(turned, -offset, axis=1).reshape(width, blocks, BAND)  63.9 us
    sub x32, other arithmetic, column_sweep(): rolled - (products * scaled[None, :])[:, :, None] * rolled_v[None, :, :]  58.7 us
    concatenate x32, other arithmetic, column_sweep(): rolled = jnp.roll(turned, -offset, axis=1).reshape(width, blocks, BAND)  50.8 us
    dynamic_slice x64, local copies, waits for them, and re-layouts, advance(): return column_sweep(state, whole_v[sweep_idx], starts[sweep_idx])  47.4 us
    all_to_all x1, blocking collectives, per_device(): lax.all_to_all(crossed.T, 'rows', split_axis=0, concat_axis=1, tiled=True)  21.6 us
  transfers between devices with their start and end apart: 16, of which 15 were waited for; matrix products, arithmetic and copies ran while one was open for 1% of the time, Pallas kernels for 0%

profile of v1, /device:TPU:0, one launch (start us, length us, event | category | flops | bytes accessed | tf_op | source)
XLA Modules:
  0.0 589.3 jit_solution(9062738321326929137)
XLA Ops:
  0.0 2.2 all_gather.3
  2.2 2.9 collective-permute-start
  5.0 5.9 collective-permute-done
  10.9 7.5 %collective-permute-done.1 = f32[32,256]{1,0:T(8,128)S(1)} collective-permute-done((f32[32,256]{1,0:T(8,128)S(1)}, f32[32,256]{1,0:T(8,128)S(1)}, u32[]{:S(2)}, u32[]{:S(2)}) %collective-permute-start.1) | collective-permute-done | bytes 32800 | tf_op jit(solution)/shard_map/ppermute | solution.py:30
  18.4 7.5 %collective-permute-done.2 = f32[32,256]{1,0:T(8,128)S(1)} collective-permute-done((f32[32,256]{1,0:T(8,128)S(1)}, f32[32,256]{1,0:T(8,128)S(1)}, u32[]{:S(2)}, u32[]{:S(2)}) %collective-permute-start.2) | collective-permute-done | bytes 32800 | tf_op jit(solution)/shard_map/ppermute | solution.py:30
  26.0 7.5 %collective-permute-done.3 = f32[32,256]{1,0:T(8,128)S(1)} collective-permute-done((f32[32,256]{1,0:T(8,128)S(1)}, f32[32,256]{1,0:T(8,128)S(1)}, u32[]{:S(2)}, u32[]{:S(2)}) %collective-permute-start.3) | collective-permute-done | bytes 32800 | tf_op jit(solution)/shard_map/ppermute | solution.py:30
  33.5 7.5 %collective-permute-done.4 = f32[32,256]{1,0:T(8,128)S(1)} collective-permute-done((f32[32,256]{1,0:T(8,128)S(1)}, f32[32,256]{1,0:T(8,128)S(1)}, u32[]{:S(2)}, u32[]{:S(2)}) %collective-permute-start.4) | collective-permute-done | bytes 32800 | tf_op jit(solution)/shard_map/ppermute | solution.py:30
  41.0 7.8 %collective-permute-done.5 = f32[32,256]{1,0:T(8,128)S(1)} collective-permute-done((f32[32,256]{1,0:T(8,128)S(1)}, f32[32,256]{1,0:T(8,128)S(1)}, u32[]{:S(2)}, u32[]{:S(2)}) %collective-permute-start.5) | collective-permute-done | bytes 32800 | tf_op jit(solution)/shard_map/ppermute | solution.py:30
  48.8 7.5 %collective-permute-done.6 = f32[32,256]{1,0:T(8,128)S(1)} collective-permute-done((f32[32,256]{1,0:T(8,128)S(1)}, f32[32,256]{1,0:T(8,128)S(1)}, u32[]{:S(2)}, u32[]{:S(2)}) %collective-permute-start.6) | collective-permute-done | bytes 32800 | tf_op jit(solution)/shard_map/ppermute | solution.py:30
  56.3 7.5 %collective-permute-done.7 = f32[32,256]{1,0:T(8,128)S(1)} collective-permute-done((f32[32,256]{1,0:T(8,128)S(1)}, f32[32,256]{1,0:T(8,128)S(1)}, u32[]{:S(2)}, u32[]{:S(2)}) %collective-permute-start.7) | collective-permute-done | bytes 32800 | tf_op jit(solution)/shard_map/ppermute | solution.py:30
  63.8 7.5 %collective-permute-done.8 = f32[32,256]{1,0:T(8,128)S(1)} collective-permute-done((f32[32,256]{1,0:T(8,128)S(1)}, f32[32,256]{1,0:T(8,128)S(1)}, u32[]{:S(2)}, u32[]{:S(2)}) %collective-permute-start.8) | collective-permute-done | bytes 32800 | tf_op jit(solution)/shard_map/ppermute | solution.py:30
  71.3 7.5 %collective-permute-done.9 = f32[32,256]{1,0:T(8,128)S(1)} collective-permute-done((f32[32,256]{1,0:T(8,128)S(1)}, f32[32,256]{1,0:T(8,128)S(1)}, u32[]{:S(2)}, u32[]{:S(2)}) %collective-permute-start.9) | collective-permute-done | bytes 32800 | tf_op jit(solution)/shard_map/ppermute | solution.py:30
  78.8 7.5 %collective-permute-done.10 = f32[32,256]{1,0:T(8,128)S(1)} collective-permute-done((f32[32,256]{1,0:T(8,128)S(1)}, f32[32,256]{1,0:T(8,128)S(1)}, u32[]{:S(2)}, u32[]{:S(2)}) %collective-permute-start.10) | collective-permute-done | bytes 32800 | tf_op jit(solution)/shard_map/ppermute | solution.py:30
  86.3 7.6 %collective-permute-done.11 = f32[32,256]{1,0:T(8,128)S(1)} collective-permute-done((f32[32,256]{1,0:T(8,128)S(1)}, f32[32,256]{1,0:T(8,128)S(1)}, u32[]{:S(2)}, u32[]{:S(2)}) %collective-permute-start.11) | collective-permute-done | bytes 32800 | tf_op jit(solution)/shard_map/ppermute | solution.py:30
  94.0 7.5 %collective-permute-done.12 = f32[32,256]{1,0:T(8,128)S(1)} collective-permute-done((f32[32,256]{1,0:T(8,128)S(1)}, f32[32,256]{1,0:T(8,128)S(1)}, u32[]{:S(2)}, u32[]{:S(2)}) %collective-permute-start.12) | collective-permute-done | bytes 32800 | tf_op jit(solution)/shard_map/ppermute | solution.py:30
  101.5 7.7 %collective-permute-done.13 = f32[32,256]{1,0:T(8,128)S(1)} collective-permute-done((f32[32,256]{1,0:T(8,128)S(1)}, f32[32,256]{1,0:T(8,128)S(1)}, u32[]{:S(2)}, u32[]{:S(2)}) %collective-permute-start.13) | collective-permute-done | bytes 32800 | tf_op jit(solution)/shard_map/ppermute | solution.py:30
  109.2 2.5 copy.12
  111.7 7.0 %all-to-all-start = ((f32[256,16,64]{0,2,1:T(8,128)}), f32[256,16,64]{0,2,1:T(8,128)S(1)}, u32[]{:S(2)}, u32[]{:S(2)}) async-start(f32[256,16,64]{0,2,1:T(8,128)} %bitcast.2), calls=%async_computation | async-start | bytes 2097152 | tf_op jit(solution)/shard_map/all_to_all | solution.py:27
  120.0 14.3 %all-to-all-done = f32[256,16,64]{0,2,1:T(8,128)S(1)} async-done(((f32[256,16,64]{0,2,1:T(8,128)}), f32[256,16,64]{0,2,1:T(8,128)S(1)}, u32[]{:S(2)}, u32[]{:S(2)}) %all-to-all-start) | async-done | bytes 1048608 | tf_op jit(solution)/shard_map/all_to_all | solution.py:27
  134.5 431.8 %while.15 = (s32[]{:T(128)}, f32[64,4096]{1,0:T(8,128)S(1)}, s32[32]{0:T(128)S(1)}, f32[32,4096]{1,0:T(8,128)}, s32[]{:T(128)}, /*index=5*/s32[]{:T(128)}, s32[]{:T(128)}, s32[]{:T(128)}, s32[]{:T(128)}) while((s32[]{:T(128)}, f32[64,4096]{1,0:T(8,128)S(1)}, s32[32]{0:T(128)S(1)}, f32[32,4096]{1,0:T(8,128)}, s32[]{:T(128)}, ...), condition=%wide.region_3.5_spmd, body=%wide.region_0.4_spmd.sunk | while | flops 1847711 | bytes 13845943 | solution.py:39
  138.9 2.0 reshape.75
  152.4 2.0 reshape.75
  165.9 2.0 reshape.75
  179.3 2.0 reshape.75
  192.8 2.0 reshape.75
  206.3 2.0 reshape.75
  219.8 2.0 reshape.75
  233.3 2.0 reshape.75
  287.3 2.0 reshape.75
  462.8 2.0 reshape.75
  543.7 2.0 reshape.75
  566.4 21.6 %all_to_all.38 = f32[16,256,64]{1,2,0:T(8,128)S(1)} all-to-all(f32[16,256,64]{1,2,0:T(8,128)S(1)} %bitcast.23), channel_id=1, replica_groups=mesh['rows'=16,'cols'=2] {'rows'}, dimensions={0} | all-to-all | bytes 2097152 | tf_op jit(solution)/shard_map/all_to_all | solution.py:40
  (490 shorter events, 339.3 us)
Async XLA Ops:
  2.2 8.8 %collective-permute-start = (f32[32,256]{1,0:T(8,128)S(1)}, f32[32,256]{1,0:T(8,128)S(1)}, u32[]{:S(2)}, u32[]{:S(2)}) collective-permute-start(f32[32,256]{1,0:T(8,128)S(1)} %all_gather.3), channel_id=1, source_target_pairs={{0,2},{2,4},{4,6},{6,8},{8,10},{10,12},{12,14},{14,16},{16,18},{18... | collective-permute-start | bytes 98312 | tf_op jit(solution)/shard_map/ppermute | solution.py:30
  10.9 7.5 %collective-permute-start.1 = (f32[32,256]{1,0:T(8,128)S(1)}, f32[32,256]{1,0:T(8,128)S(1)}, u32[]{:S(2)}, u32[]{:S(2)}) collective-permute-start(f32[32,256]{1,0:T(8,128)S(1)} %collective-permute-done), channel_id=1, source_target_pairs={{0,2},{2,4},{4,6},{6,8},{8,10},{10,12},{12,14},{14,16},{16,18},{18... | collective-permute-start | bytes 98312 | tf_op jit(solution)/shard_map/ppermute | solution.py:30
  18.4 7.5 %collective-permute-start.2 = (f32[32,256]{1,0:T(8,128)S(1)}, f32[32,256]{1,0:T(8,128)S(1)}, u32[]{:S(2)}, u32[]{:S(2)}) collective-permute-start(f32[32,256]{1,0:T(8,128)S(1)} %collective-permute-done.1), channel_id=1, source_target_pairs={{0,2},{2,4},{4,6},{6,8},{8,10},{10,12},{12,14},{14,16},{16,18},{18... | collective-permute-start | bytes 98312 | tf_op jit(solution)/shard_map/ppermute | solution.py:30
  25.9 7.5 %collective-permute-start.3 = (f32[32,256]{1,0:T(8,128)S(1)}, f32[32,256]{1,0:T(8,128)S(1)}, u32[]{:S(2)}, u32[]{:S(2)}) collective-permute-start(f32[32,256]{1,0:T(8,128)S(1)} %collective-permute-done.2), channel_id=1, source_target_pairs={{0,2},{2,4},{4,6},{6,8},{8,10},{10,12},{12,14},{14,16},{16,18},{18... | collective-permute-start | bytes 98312 | tf_op jit(solution)/shard_map/ppermute | solution.py:30
  33.5 7.5 %collective-permute-start.4 = (f32[32,256]{1,0:T(8,128)S(1)}, f32[32,256]{1,0:T(8,128)S(1)}, u32[]{:S(2)}, u32[]{:S(2)}) collective-permute-start(f32[32,256]{1,0:T(8,128)S(1)} %collective-permute-done.3), channel_id=1, source_target_pairs={{0,2},{2,4},{4,6},{6,8},{8,10},{10,12},{12,14},{14,16},{16,18},{18... | collective-permute-start | bytes 98312 | tf_op jit(solution)/shard_map/ppermute | solution.py:30
  41.0 7.8 %collective-permute-start.5 = (f32[32,256]{1,0:T(8,128)S(1)}, f32[32,256]{1,0:T(8,128)S(1)}, u32[]{:S(2)}, u32[]{:S(2)}) collective-permute-start(f32[32,256]{1,0:T(8,128)S(1)} %collective-permute-done.4), channel_id=1, source_target_pairs={{0,2},{2,4},{4,6},{6,8},{8,10},{10,12},{12,14},{14,16},{16,18},{18... | collective-permute-start | bytes 98312 | tf_op jit(solution)/shard_map/ppermute | solution.py:30
  48.8 7.5 %collective-permute-start.6 = (f32[32,256]{1,0:T(8,128)S(1)}, f32[32,256]{1,0:T(8,128)S(1)}, u32[]{:S(2)}, u32[]{:S(2)}) collective-permute-start(f32[32,256]{1,0:T(8,128)S(1)} %collective-permute-done.5), channel_id=1, source_target_pairs={{0,2},{2,4},{4,6},{6,8},{8,10},{10,12},{12,14},{14,16},{16,18},{18... | collective-permute-start | bytes 98312 | tf_op jit(solution)/shard_map/ppermute | solution.py:30
  56.3 7.5 %collective-permute-start.7 = (f32[32,256]{1,0:T(8,128)S(1)}, f32[32,256]{1,0:T(8,128)S(1)}, u32[]{:S(2)}, u32[]{:S(2)}) collective-permute-start(f32[32,256]{1,0:T(8,128)S(1)} %collective-permute-done.6), channel_id=1, source_target_pairs={{0,2},{2,4},{4,6},{6,8},{8,10},{10,12},{12,14},{14,16},{16,18},{18... | collective-permute-start | bytes 98312 | tf_op jit(solution)/shard_map/ppermute | solution.py:30
  63.8 7.5 %collective-permute-start.8 = (f32[32,256]{1,0:T(8,128)S(1)}, f32[32,256]{1,0:T(8,128)S(1)}, u32[]{:S(2)}, u32[]{:S(2)}) collective-permute-start(f32[32,256]{1,0:T(8,128)S(1)} %collective-permute-done.7), channel_id=1, source_target_pairs={{0,2},{2,4},{4,6},{6,8},{8,10},{10,12},{12,14},{14,16},{16,18},{18... | collective-permute-start | bytes 98312 | tf_op jit(solution)/shard_map/ppermute | solution.py:30
  71.3 7.5 %collective-permute-start.9 = (f32[32,256]{1,0:T(8,128)S(1)}, f32[32,256]{1,0:T(8,128)S(1)}, u32[]{:S(2)}, u32[]{:S(2)}) collective-permute-start(f32[32,256]{1,0:T(8,128)S(1)} %collective-permute-done.8), channel_id=1, source_target_pairs={{0,2},{2,4},{4,6},{6,8},{8,10},{10,12},{12,14},{14,16},{16,18},{18... | collective-permute-start | bytes 98312 | tf_op jit(solution)/shard_map/ppermute | solution.py:30
  78.8 7.5 %collective-permute-start.10 = (f32[32,256]{1,0:T(8,128)S(1)}, f32[32,256]{1,0:T(8,128)S(1)}, u32[]{:S(2)}, u32[]{:S(2)}) collective-permute-start(f32[32,256]{1,0:T(8,128)S(1)} %collective-permute-done.9), channel_id=1, source_target_pairs={{0,2},{2,4},{4,6},{6,8},{8,10},{10,12},{12,14},{14,16},{16,18},{18... | collective-permute-start | bytes 98312 | tf_op jit(solution)/shard_map/ppermute | solution.py:30
  86.3 7.6 %collective-permute-start.11 = (f32[32,256]{1,0:T(8,128)S(1)}, f32[32,256]{1,0:T(8,128)S(1)}, u32[]{:S(2)}, u32[]{:S(2)}) collective-permute-start(f32[32,256]{1,0:T(8,128)S(1)} %collective-permute-done.10), channel_id=1, source_target_pairs={{0,2},{2,4},{4,6},{6,8},{8,10},{10,12},{12,14},{14,16},{16,18},{18... | collective-permute-start | bytes 98312 | tf_op jit(solution)/shard_map/ppermute | solution.py:30
  94.0 7.5 %collective-permute-start.12 = (f32[32,256]{1,0:T(8,128)S(1)}, f32[32,256]{1,0:T(8,128)S(1)}, u32[]{:S(2)}, u32[]{:S(2)}) collective-permute-start(f32[32,256]{1,0:T(8,128)S(1)} %collective-permute-done.11), channel_id=1, source_target_pairs={{0,2},{2,4},{4,6},{6,8},{8,10},{10,12},{12,14},{14,16},{16,18},{18... | collective-permute-start | bytes 98312 | tf_op jit(solution)/shard_map/ppermute | solution.py:30
  101.5 7.7 %collective-permute-start.13 = (f32[32,256]{1,0:T(8,128)S(1)}, f32[32,256]{1,0:T(8,128)S(1)}, u32[]{:S(2)}, u32[]{:S(2)}) collective-permute-start(f32[32,256]{1,0:T(8,128)S(1)} %collective-permute-done.12), channel_id=1, source_target_pairs={{0,2},{2,4},{4,6},{6,8},{8,10},{10,12},{12,14},{14,16},{16,18},{18... | collective-permute-start | bytes 98312 | tf_op jit(solution)/shard_map/ppermute | solution.py:30
  109.2 9.6 %collective-permute-start.14 = (f32[32,256]{1,0:T(8,128)S(1)}, f32[32,256]{1,0:T(8,128)S(1)}, u32[]{:S(2)}, u32[]{:S(2)}) collective-permute-start(f32[32,256]{1,0:T(8,128)S(1)} %collective-permute-done.13), channel_id=1, source_target_pairs={{0,2},{2,4},{4,6},{6,8},{8,10},{10,12},{12,14},{14,16},{16,18},{18... | collective-permute-start | bytes 98312 | tf_op jit(solution)/shard_map/ppermute | solution.py:30
  111.7 22.6 %all-to-all-start = ((f32[256,16,64]{0,2,1:T(8,128)}), f32[256,16,64]{0,2,1:T(8,128)S(1)}, u32[]{:S(2)}, u32[]{:S(2)}) async-start(f32[256,16,64]{0,2,1:T(8,128)} %bitcast.2), calls=%async_computation | async-start | bytes 2097152 | tf_op jit(solution)/shard_map/all_to_all | solution.py:27
  119.0 15.5 %copy-start = (s32[32]{0:T(128)S(1)}, s32[32]{0:T(128)}, u32[]{:S(2)}) copy-start(s32[32]{0:T(128)} %param.9) | copy-start | bytes 388
